TPU v7x, 256 devices: a whole 4x4x8 slice. The times are simulated.
256 devices in a mesh: angle: 2 (over y_hi), ty: 16 (over z, core), tx: 8 (over x, y_lo).
Axes of the slice: x: 4, y: 4 (y_hi: 2, y_lo: 2; y = y_hi * 2 + y_lo), z: 8, core: 2. Of those that a mesh axis runs over, the one named last changes fastest.
Arguments:
- object_slices: float32 [2, 2, 4096, 8192], P('angle', None, 'ty', 'tx'), may hold values from -5 to 5
- probe_field: float32 [2, 256, 256], replicated, may hold values from -6 to 6
- positions: int32 [2, 16, 8, 4, 2], P('angle', 'ty', 'tx'), may hold values from 0 to 7936, as said below
- live_slots: int32 [2, 16, 8], P('angle', 'ty', 'tx'), may hold values from 1 to 4, as said below
- photon_counts: int32 [2, 16, 8, 4, 256, 256], P('angle', 'ty', 'tx'), may hold values from 1 to 1600
Outputs:
- new_object: float32 [2, 2, 4096, 8192], P('angle', None, 'ty', 'tx')
- new_probe: float32 [2, 256, 256], P(None, 'ty')
Inputs may be any that keep to these rules, and one draw needn't show every extreme that they name: `positions`: A slot's patch lies inside the object and its centre (top-left plus 128) lies in the rows and columns of the tile that holds the slot: rows r * 256 to (r + 1) * 256 - 1, columns c * 1024 to (c + 1) * 1024 - 1. `live_slots`: some tile of every draw uses all 4 slots.
All inputs are finite; a program needn't handle non-finite values.
Results may differ from a plain program's by a relative error of at most 0.0003.
Values sent between devices are 32-bit elements; how exact they have to be, the bound alone decides.
A program may use at most 128 MiB of HBM per device.

v0:
```python
import functools
import math

import jax
import jax.numpy as jnp
import numpy as np
from jax import lax
from jax.experimental import pallas as pl
from jax.experimental.pallas import tpu as pltpu
from jax.sharding import PartitionSpec as P

MESH = pl.DeviceIdType.MESH
F32 = jnp.float32
BF16 = jnp.bfloat16
SIZE = 256
HALF = 128
TR = 256
TC = 1024
WR = TR + SIZE
WC = TC + SIZE
N_TY = 16
N_TX = 8
N_ANGLE = 2
N_XY = N_ANGLE * N_TX


def tables():
    n = np.arange(HALF)
    base = np.exp(-2j * np.pi * np.outer(n, n) / HALF) / 16.0
    odd = base * np.exp(-2j * np.pi * n / SIZE)[None, :]

    def real_form(m):
        return np.block([[m.real, -m.imag], [m.imag, m.real]])

    mats = [real_form(base), real_form(odd)]
    mats = np.stack([mats[0], mats[1], mats[0].T, mats[1].T]).astype(np.float32)
    high = mats.astype(jnp.bfloat16)
    low = (mats - high.astype(np.float32)).astype(jnp.bfloat16)
    order = np.zeros((SIZE, SIZE), np.float32)
    for j in range(SIZE):
        order[2 * j if j < HALF else 2 * (j - HALF) + 1, j] = 1.0
    both = np.stack([order, order.T]).astype(jnp.bfloat16)
    return high, low, both


TABLE_HIGH, TABLE_LOW, TABLE_ORDER = tables()


def remote(src, dst, send, recv, **where):
    return pltpu.make_async_remote_copy(
        src_ref=src, dst_ref=dst, send_sem=send, recv_sem=recv, device_id=where, device_id_type=MESH
    )


def split(x):
    high = x.astype(BF16)
    return high, (x - high.astype(F32)).astype(BF16)


def dot(a, b):
    return jnp.dot(a, b, preferred_element_type=F32)


class Copies:
    def __init__(self, send, recv):
        self.send, self.recv, self.at = send, recv, 0

    def make(self, src, dst, **where):
        copy = remote(src, dst, self.send.at[self.at], self.recv.at[self.at], **where)
        self.at += 1
        return copy


def step_kernel(
    tile, meta, probe_h, counts_h, high_h, low_h, order_h, new_tile, new_probe,
    wide, probe, counts, high, low, order, around, around_s, padded, den, patches,
    canvas, vin, cin, hin, hout, pk_own, pk_xy, pk, pk_ty,
    den_sums, den_pair, den_mine, den_box, den_part, den_zbox, den_final, den_whole,
    num_sums, num_pair, num_mine, num_box, num_part, num_zbox, num_final, num_whole,
    send, recv, local,
):
    angle, ty, tx = lax.axis_index("angle"), lax.axis_index("ty"), lax.axis_index("tx")
    up, down = lax.rem(ty + N_TY - 1, N_TY), lax.rem(ty + 1, N_TY)
    left, right = lax.rem(tx + N_TX - 1, N_TX), lax.rem(tx + 1, N_TX)
    me = angle * N_TX + tx
    core, z = lax.rem(ty, 2), ty // 2
    goal, half = me // 2, lax.rem(me, 2)
    copies = Copies(send, recv)

    def xy_peer(step):
        other = lax.rem(me + step, N_XY)
        return other, {"angle": other // N_TX, "tx": lax.rem(other, N_TX)}

    def ty_peer(step):
        return {"ty": lax.rem(ty + step, N_TY)}

    barrier = pltpu.get_barrier_semaphore()
    for step in range(1, 16):
        pl.semaphore_signal(barrier, inc=1, device_id=xy_peer(step)[1], device_id_type=MESH)
        pl.semaphore_signal(barrier, inc=1, device_id=ty_peer(step), device_id_type=MESH)

    middle_blocks, middle_groups = pl.ds(1, 8), pl.ds(16, 32)
    top_in, bottom_in = pl.ds(16, 16), pl.ds(32, 16)
    top_out, bottom_out = pl.ds(0, 16), pl.ds(48, 16)
    middle = [
        pltpu.make_async_copy(
            tile.at[:, :, :, pl.ds(block * HALF, HALF)], wide.at[1 + block, :, middle_groups], local.at[10 + block]
        )
        for block in range(8)
    ]
    own = pltpu.make_async_copy(meta, around.at[1, 1], local.at[1])
    loads = [
        pltpu.make_async_copy(src, dst, local.at[2 + k])
        for k, (src, dst) in enumerate(
            ((probe_h, probe), (high_h, high), (low_h, low), (order_h, order), (counts_h, counts))
        )
    ]
    for copy in middle:
        copy.start()
    own.start()
    for load in loads:
        load.start()

    def clear(item, carry):
        padded[item // 16, lax.rem(item // 4, 4), lax.rem(item, 4)] = jnp.zeros((96, 8, HALF), F32)
        return carry

    lax.fori_loop(0, 32, clear, 0)
    own.wait()
    for copy in middle:
        copy.wait()
    pl.semaphore_wait(barrier, 30)

    meta_sides = [
        copies.make(meta, around.at[1, 2], tx=left),
        copies.make(meta, around.at[1, 0], tx=right),
    ]
    sides = [
        copies.make(wide.at[1, :, middle_groups], wide.at[9, :, middle_groups], tx=left),
        copies.make(wide.at[8, :, middle_groups], wide.at[0, :, middle_groups], tx=right),
    ]
    ends = [
        copies.make(wide.at[middle_blocks, :, top_in], wide.at[middle_blocks, :, bottom_out], ty=up),
        copies.make(wide.at[middle_blocks, :, bottom_in], wide.at[middle_blocks, :, top_out], ty=down),
    ]
    for copy in meta_sides + sides + ends:
        copy.start()
    for copy in meta_sides:
        copy.wait()
    meta_ends = [
        copies.make(around.at[1], around.at[2], ty=up),
        copies.make(around.at[1], around.at[0], ty=down),
    ]
    for copy in meta_ends:
        copy.start()
    for copy in meta_ends:
        copy.wait()
    scalars = pltpu.make_async_copy(around, around_s, local.at[7])
    scalars.start()
    scalars.wait()

    lane33 = lax.broadcasted_iota(jnp.int32, (33, 8, HALF), 2)
    lane32 = lax.broadcasted_iota(jnp.int32, (32, 8, HALF), 2)
    sub33 = lax.broadcasted_iota(jnp.int32, (33, 8, HALF), 1)
    sub32 = lax.broadcasted_iota(jnp.int32, (32, 8, HALF), 1)
    blank = jnp.zeros((1, 8, HALF), F32)

    def lay(channel, slot, by_row, by_col, x):
        def turned(part):
            return pltpu.roll(pltpu.roll(part.reshape(32, 8, HALF), by_col, 2), by_row, 1)

        one, two = turned(x[:, :HALF]), turned(x[:, HALF:])
        inside = lane32 >= by_col
        below = sub33 >= by_row
        zero = jnp.zeros_like(one)
        for step, part in enumerate(
            (jnp.where(inside, one, zero), jnp.where(inside, two, one), jnp.where(inside, zero, two))
        ):
            moved = jnp.where(
                below, jnp.concatenate([part, blank], 0), jnp.concatenate([blank, part], 0)
            )
            padded[channel, slot, 1 + step, pl.ds(32, 33)] = moved

    def fetch(channel, spots, block, first, count, put):
        where = []
        for slot in range(4):
            at_group, at_block = spots[slot]
            near = block - at_block
            where.append((jnp.where((near >= 0) & (near <= 2), near + 1, 0), 32 + first - at_group))
        for step in range(count):
            total = None
            for slot, (index, start) in enumerate(where):
                part = padded[channel, slot, index, start + step]
                total = part if total is None else total + part
            put(step, total)

    def group(dy, dx, begin):
        spots = []
        for slot in range(4):
            row = around_s[dy + 1, dx + 1, 0, 2 * slot] - ty * TR
            col = around_s[dy + 1, dx + 1, 0, 2 * slot + 1] - tx * TC
            used = slot < around_s[dy + 1, dx + 1, 0, 8]
            near = (row > -SIZE) & (row < TR) & (col > -SIZE) & (col < TC)
            weight = jnp.where(used & near, 1.0, 0.0).astype(F32)
            row = jnp.clip(row, -SIZE, TR - 1) + SIZE
            col = jnp.clip(col, -SIZE, TC - 1) + SIZE
            at_group, by_row = row // 8, lax.rem(row, 8)
            at_block, by_col = col // HALF, lax.rem(col, HALF)
            qr, qi = probe[0], probe[1]
            lay(0, slot, by_row, by_col, (qr * qr + qi * qi) * weight)
            spots.append((at_group - 32, at_block - 2))
        first, count = {-1: (0, 16), 0: (0, 32), 1: (16, 16)}[dy]
        begin_block, end_block = {-1: (0, 1), 0: (0, 8), 1: (7, 8)}[dx]

        def one_block(block, carry):
            def put(step, total):
                if begin:
                    den[block, first + step] = total
                else:
                    den[block, first + step] += total

            fetch(0, spots, block, first, count, put)
            return carry

        lax.fori_loop(begin_block, end_block, one_block, 0)

    loads[0].wait()
    group(0, 0, True)
    for dy, dx in ((-1, 0), (1, 0), (0, -1), (0, 1)):
        group(dy, dx, False)
    corners = []
    for side, block in ((0, 0), (1, 9)):
        sides[1 - side].wait_recv()
        for src, dst, where in ((top_in, bottom_out, {"ty": up}), (bottom_in, top_out, {"ty": down})):
            corners.append(copies.make(wide.at[block, :, src], wide.at[block, :, dst], **where))
            corners[-1].start()
    for dy, dx in ((-1, -1), (-1, 1), (1, -1), (1, 1)):
        group(dy, dx, False)
    pk_own[...] = jnp.broadcast_to(jnp.max(den[...]), (8, HALF))
    pk_copies = []
    for step in range(1, 16):
        pk_copies.append(copies.make(pk_own, pk_xy.at[step], **xy_peer(step)[1]))
        pk_copies[-1].start()
    for side in sides:
        side.wait_send()
    for copy in ends + corners:
        copy.wait()

    den_sums[...] = jnp.zeros_like(den_sums)
    num_sums[...] = jnp.zeros_like(num_sums)

    def place_of(slot):
        row = jnp.clip(around_s[1, 1, 0, 2 * slot] - (ty * TR - HALF), 0, TR - 1)
        col = jnp.clip(around_s[1, 1, 0, 2 * slot + 1] - (tx * TC - HALF), 0, TC - 1)
        return row // 8, lax.rem(row, 8), col // HALF, lax.rem(col, HALF)

    def weight_of(slot):
        return jnp.where(slot < around_s[1, 1, 0, 8], 1.0, 0.0).astype(F32)

    def add_rows(sums, channel, x):
        x = x.reshape(8, 2, 2, 8, SIZE)
        for parity in range(2):
            sums[parity, :, channel] += x[:, parity].reshape(16, 8, SIZE)

    def cut(slot, carry):
        at_group, by_row, at_block, by_col = place_of(slot)
        back_row, back_col = lax.rem(8 - by_row, 8), lax.rem(HALF - by_col, HALF)
        power = None
        for channel in range(2):
            parts = []
            for step in range(3):
                x = jnp.stack([wide[at_block + step, channel, at_group + k] for k in range(33)])
                parts.append(pltpu.roll(x, back_col, 2))
            done = []
            for step in range(2):
                x = jnp.where(lane33 < HALF - by_col, parts[step], parts[step + 1])
                x = pltpu.roll(x, back_row, 1)
                x = jnp.where(sub32 < 8 - by_row, x[:32], x[1:])
                done.append(x.reshape(SIZE, HALF))
            x = jnp.concatenate(done, 1)
            patches[slot, channel] = x
            power = x * x if power is None else power + x * x
        add_rows(den_sums, 0, power * weight_of(slot))
        return carry

    lax.fori_loop(0, 4, cut, 0)

    class Chain:
        def __init__(self, sums, pair, mine, box, part, zbox, final, whole, sem):
            self.__dict__.update(
                sums=sums, pair=pair, mine=mine, box=box, part=part, zbox=zbox, final=final, whole=whole
            )
            self.keep = pltpu.make_async_copy(final, whole.at[half], local.at[sem])
            self.over_pair = copies.make(sums.at[1 - core], pair, ty=ty + 1 - 2 * core)
            self.over_xy = [
                copies.make(mine.at[xy_peer(step)[0]], box.at[step], **xy_peer(step)[1]) for step in range(1, 16)
            ]
            base = copies.at
            far = lax.rem(goal - z + 8, 8)
            self.to_goal = remote(part, zbox.at[far], send.at[base], recv.at[base + far], ty=2 * goal + core)
            self.at_goal = [
                remote(part, zbox.at[step], send.at[base], recv.at[base + step], ty=up) for step in range(1, 8)
            ]
            base += 8
            self.out = [
                remote(final, whole.at[half], send.at[base + step], recv.at[base + half], **xy_peer(step)[1])
                for step in range(1, 16)
            ]
            self.into = [
                remote(final, whole.at[k], send.at[base], recv.at[base + k], tx=left) for k in range(2)
            ]
            copies.at = base + 16

        def start_pair(self):
            self.over_pair.start()

        def start_xy(self):
            self.over_pair.wait()
            self.mine[...] = self.sums[core] + self.pair[...]
            for copy in self.over_xy:
                copy.start()

        def start_z(self):
            for copy in self.over_xy:
                copy.wait()
            total = self.mine[me]
            for step in range(1, 16):
                total = total + self.box[step]
            self.part[...] = total

            @pl.when(z != goal)
            def _():
                self.to_goal.start()

        def start_out(self):
            @pl.when(z != goal)
            def _():
                self.to_goal.wait_send()

            @pl.when(z == goal)
            def _():
                for copy in self.at_goal:
                    copy.wait_recv()
                total = self.part[...]
                for step in range(1, 8):
                    total = total + self.zbox[step]
                self.final[...] = total
                self.keep.start()
                for copy in self.out:
                    copy.start()

        def finish(self):
            @pl.when(z == goal)
            def _():
                self.keep.wait()
                for copy in self.out:
                    copy.wait_send()

            for k in range(2):
                @pl.when(me != 2 * z + k)
                def _():
                    self.into[k].wait_recv()

    den_chain = Chain(den_sums, den_pair, den_mine, den_box, den_part, den_zbox, den_final, den_whole, 8)
    num_chain = Chain(num_sums, num_pair, num_mine, num_box, num_part, num_zbox, num_final, num_whole, 9)
    den_chain.start_pair()
    for load in loads[1:]:
        load.wait()

    def from_left(which, x):
        a, b = split(x)
        return dot(high[which], a) + (dot(high[which], b) + dot(low[which], a))

    def from_right(x, which):
        a, b = split(x)
        return dot(a, high[which]) + (dot(b, high[which]) + dot(a, low[which]))

    def one_slot(slot, carry):
        at_group, by_row, at_block, by_col = place_of(slot)
        weight = weight_of(slot)
        xr, xi = patches[slot, 0], patches[slot, 1]
        qr, qi = probe[0], probe[1]
        pr, pi = qr * xr - qi * xi, qr * xi + qi * xr
        even = from_right(
            jnp.concatenate([pr[:, :HALF] + pr[:, HALF:], pi[:, :HALF] + pi[:, HALF:]], 1), 2
        )
        odd = from_right(
            jnp.concatenate([pr[:, :HALF] - pr[:, HALF:], pi[:, :HALF] - pi[:, HALF:]], 1), 3
        )
        mr = jnp.concatenate([even[:, :HALF], odd[:, :HALF]], 1)
        mi = jnp.concatenate([even[:, HALF:], odd[:, HALF:]], 1)
        fe = from_left(0, jnp.concatenate([mr[:HALF] + mr[HALF:], mi[:HALF] + mi[HALF:]], 0))
        fo = from_left(1, jnp.concatenate([mr[:HALF] - mr[HALF:], mi[:HALF] - mi[HALF:]], 0))
        count = counts[slot]
        tens = lax.shift_right_logical(count, 4)
        ones = count - 16 * tens
        tens = dot(dot(order[1], tens.astype(F32).astype(BF16)).astype(BF16), order[0])
        ones = dot(dot(order[1], ones.astype(F32).astype(BF16)).astype(BF16), order[0])
        count = 16.0 * tens + ones

        def scaled(f, c):
            re, im = f[:HALF], f[HALF:]
            size = jnp.maximum(re * re + im * im, 0.0625)
            factor = (0.05 * c) * lax.rsqrt(c * size)
            return jnp.concatenate([re * factor, im * factor], 0)

        ge = from_left(2, scaled(fe, count[:HALF]))
        go = from_left(3, scaled(fo, count[HALF:]))
        top, bottom = ge + go, ge - go
        hr_ = jnp.concatenate([top[:HALF], bottom[:HALF]], 0)
        hi_ = jnp.concatenate([top[HALF:], bottom[HALF:]], 0)
        be = from_right(jnp.concatenate([hr_[:, :HALF], hi_[:, :HALF]], 1), 0)
        bo = from_right(jnp.concatenate([hr_[:, HALF:], hi_[:, HALF:]], 1), 1)
        first, second = be + bo, be - bo
        dr = (jnp.concatenate([first[:, :HALF], second[:, :HALF]], 1) - pr) * weight
        di = (jnp.concatenate([first[:, HALF:], second[:, HALF:]], 1) - pi) * weight
        lay(0, slot, by_row, by_col, qr * dr + qi * di)
        lay(1, slot, by_row, by_col, qr * di - qi * dr)
        add_rows(num_sums, 0, xr * dr + xi * di)
        add_rows(num_sums, 1, xr * di - xi * dr)
        return carry

    lax.fori_loop(0, 1, one_slot, 0)
    den_chain.start_xy()
    lax.fori_loop(1, 4, one_slot, 0)
    num_chain.start_pair()

    places = [(place_of(slot)[0], place_of(slot)[2]) for slot in range(4)]

    def one_canvas(block, carry):
        for channel in range(2):
            def put(step, total):
                canvas[block, channel, step] = total

            fetch(channel, places, block, 0, 64, put)
        return carry

    lax.fori_loop(0, 2, lambda k, carry: one_canvas(9 * k, carry), 0)
    back_corners = []
    for side, block in ((0, 0), (1, 9)):
        for way, (src, where) in enumerate(((top_out, {"ty": up}), (bottom_out, {"ty": down}))):
            back_corners.append(copies.make(canvas.at[block, :, src], cin.at[2 * side + way], **where))
            back_corners[-1].start()
    lax.fori_loop(1, 9, one_canvas, 0)
    back_ends = [
        [
            copies.make(canvas.at[middle_blocks, channel, top_out], vin.at[0, channel], ty=up),
            copies.make(canvas.at[middle_blocks, channel, bottom_out], vin.at[1, channel], ty=down),
        ]
        for channel in range(2)
    ]
    for copy in back_ends[0]:
        copy.start()
    den_chain.start_z()
    num_chain.start_xy()
    for copy in back_corners:
        copy.wait()
    for side, block in ((0, 0), (1, 9)):
        hout[side, :, pl.ds(0, 16)] = canvas[block, :, top_in] + cin[2 * side + 1]
        hout[side, :, pl.ds(16, 16)] = canvas[block, :, bottom_in] + cin[2 * side]
    across = [
        copies.make(hout.at[0], hin.at[0], tx=left),
        copies.make(hout.at[1], hin.at[1], tx=right),
    ]
    for copy in across:
        copy.start()
    den_chain.start_out()
    num_chain.start_z()
    for copy in back_ends[1]:
        copy.start()
    for copy in pk_copies:
        copy.wait()
    top = pk_own[...]
    for step in range(1, 16):
        top = jnp.maximum(top, pk_xy[step])
    pk[0] = top
    den_chain.finish()
    pk[1] = jnp.broadcast_to(jnp.max(den_whole[...]), (8, HALF))
    pk_copies = []
    for step in range(1, 16):
        pk_copies.append(copies.make(pk, pk_ty.at[step], **ty_peer(step)))
        pk_copies[-1].start()
    num_chain.start_out()
    for copy in pk_copies:
        copy.wait()
    top = pk[...]
    for step in range(1, 16):
        top = jnp.maximum(top, pk_ty[step])
    peak_obj, peak_probe = top[0, 0, 0], top[1, 0, 0]
    den[...] = 1.0 / (den[...] + 0.1 * peak_obj)
    for copy in across:
        copy.wait()
    for block, side in ((8, 0), (1, 1)):
        canvas[block, :, middle_groups] += hin[side]
    for channel in range(2):
        for copy in back_ends[channel]:
            copy.wait()
        for first, side in ((0, 1), (16, 0)):
            here, there = pl.ds(16 + first, 16), pl.ds(first, 16)
            for block in range(8):
                value = canvas[1 + block, channel, here] + vin[side, channel, block]
                new_tile[channel, there, :, pl.ds(block * HALF, HALF)] = (
                    wide[1 + block, channel, here] + value * den[block, there]
                )
    num_chain.finish()
    for k in range(2):
        rows = pl.ds(pl.multiple_of(16 * ty + 8 * k, 8), 8)
        scale = 1.0 / (den_whole[k, 0] + 0.1 * peak_probe)
        for channel in range(2):
            new_probe[channel, pl.ds(8 * k, 8)] = probe[channel, rows, :] + num_whole[k, channel] * scale


def vmem():
    return pl.BlockSpec(memory_space=pltpu.VMEM)


def chain_scratch(channels):
    piece = (channels, 8, SIZE)
    shapes = ((2, 16) + piece, (16,) + piece, (16,) + piece, (16,) + piece, piece, (8,) + piece, piece, (2,) + piece)
    return [pltpu.VMEM(shape, F32) for shape in shapes]


def body(object_slices, probe_field, positions, live_slots, photon_counts):
    line = jnp.concatenate([positions.reshape(-1), live_slots.reshape(-1)])
    meta = jnp.pad(line, (0, HALF - 9)).reshape(1, HALF)
    small = (8, HALF)
    new_tile, new_probe = pl.pallas_call(
        step_kernel,
        name="step",
        out_shape=(
            jax.ShapeDtypeStruct((2, 32, 8, TC), F32),
            jax.ShapeDtypeStruct((2, 16, SIZE), F32),
        ),
        in_specs=[pl.BlockSpec(memory_space=pltpu.HBM), vmem()] + [pl.BlockSpec(memory_space=pltpu.HBM)] * 5,
        out_specs=(vmem(), vmem()),
        scratch_shapes=[
            pltpu.VMEM((10, 2, 64, 8, HALF), F32),
            pltpu.VMEM((2, SIZE, SIZE), F32),
            pltpu.VMEM((4, SIZE, SIZE), jnp.int32),
            pltpu.VMEM((4, SIZE, SIZE), BF16),
            pltpu.VMEM((4, SIZE, SIZE), BF16),
            pltpu.VMEM((2, SIZE, SIZE), BF16),
            pltpu.VMEM((3, 3, 1, HALF), jnp.int32),
            pltpu.SMEM((3, 3, 1, HALF), jnp.int32),
            pltpu.VMEM((2, 4, 4, 96, 8, HALF), F32),
            pltpu.VMEM((8, 32, 8, HALF), F32),
            pltpu.VMEM((4, 2, SIZE, SIZE), F32),
            pltpu.VMEM((10, 2, 64, 8, HALF), F32),
            pltpu.VMEM((2, 2, 8, 16, 8, HALF), F32),
            pltpu.VMEM((4, 2, 16, 8, HALF), F32),
            pltpu.VMEM((2, 2, 32, 8, HALF), F32),
            pltpu.VMEM((2, 2, 32, 8, HALF), F32),
            pltpu.VMEM(small, F32),
            pltpu.VMEM((16,) + small, F32),
            pltpu.VMEM((2,) + small, F32),
            pltpu.VMEM((16, 2) + small, F32),
            *chain_scratch(1),
            *chain_scratch(2),
            pltpu.SemaphoreType.DMA((144,)),
            pltpu.SemaphoreType.DMA((144,)),
            pltpu.SemaphoreType.DMA((18,)),
        ],
        compiler_params=pltpu.CompilerParams(
            collective_id=0, has_side_effects=True, vmem_limit_bytes=46 << 20
        ),
    )(
        object_slices.reshape(2, 32, 8, TC), meta, probe_field, photon_counts[0, 0, 0],
        jnp.asarray(TABLE_HIGH), jnp.asarray(TABLE_LOW), jnp.asarray(TABLE_ORDER),
    )
    return (new_tile.reshape(1, 2, TR, TC), new_probe)


def solution(mesh):
    placed = (
        P("angle", None, "ty", "tx"),
        P(),
        P("angle", "ty", "tx", None, None),
        P("angle", "ty", "tx"),
        P("angle", "ty", "tx", None, None, None),
    )
    return jax.shard_map(
        body,
        mesh=mesh,
        in_specs=placed,
        out_specs=(P("angle", None, "ty", "tx"), P(None, "ty", None)),
        check_vma=False,
    )
```

profile of v0, /device:TPU:1, one launch (start us, length us, event | category | flops | bytes accessed | tf_op | source)
XLA Modules:
  0.0 85.0 jit_solution(5987418027220402516)
XLA Ops:
  1.3 0.8 copy.11
  2.0 0.1 reshape.20
  2.1 0.1 pad_add_fusion
  2.2 0.0 copy-start
  2.2 1.6 %copy-done = f32[1,2,256,1024]{3,2,1,0:T(8,128)S(1)} copy-done((f32[1,2,256,1024]{3,2,1,0:T(8,128)S(1)}, f32[1,2,256,1024]{3,2,1,0:T(8,128)}, u32[]{:S(2)}) %copy-start) | copy-done | bytes 2097176
  3.8 0.0 copy-start.1
  3.8 1.2 %copy-done.1 = s32[1,1,1,4,256,256]{5,4,3,2,1,0:T(8,128)S(1)} copy-done((s32[1,1,1,4,256,256]{5,4,3,2,1,0:T(8,128)S(1)}, s32[1,1,1,4,256,256]{5,4,3,2,1,0:T(8,128)}, u32[]{:S(2)}) %copy-start.1) | copy-done | bytes 1048600
  5.0 0.0 copy-start.2
  5.0 1.0 %copy-done.2 = f32[2,256,256]{2,1,0:T(8,128)S(1)} copy-done((f32[2,256,256]{2,1,0:T(8,128)S(1)}, f32[2,256,256]{2,1,0:T(8,128)}, u32[]{:S(2)}) %copy-start.2) | copy-done | bytes 524312
  6.1 0.0 copy-start.3
  6.1 1.0 %copy-done.3 = bf16[4,256,256]{2,1,0:T(8,128)(2,1)S(1)} copy-done((bf16[4,256,256]{2,1,0:T(8,128)(2,1)S(1)}, bf16[4,256,256]{2,1,0:T(8,128)(2,1)}, u32[]{:S(2)}) %copy-start.3) | copy-done | bytes 524312
  7.1 0.0 copy-start.4
  7.1 1.0 %copy-done.4 = bf16[4,256,256]{2,1,0:T(8,128)(2,1)S(1)} copy-done((bf16[4,256,256]{2,1,0:T(8,128)(2,1)S(1)}, bf16[4,256,256]{2,1,0:T(8,128)(2,1)}, u32[]{:S(2)}) %copy-start.4) | copy-done | bytes 524312
  8.2 0.0 copy-start.5
  8.2 0.9 %copy-done.5 = bf16[2,256,256]{2,1,0:T(8,128)(2,1)S(1)} copy-done((bf16[2,256,256]{2,1,0:T(8,128)(2,1)S(1)}, bf16[2,256,256]{2,1,0:T(8,128)(2,1)}, u32[]{:S(2)}) %copy-start.5) | copy-done | bytes 262168
  9.1 74.0 %step.1 = (f32[2,32,8,1024]{3,2,1,0:T(8,128)S(1)}, f32[2,16,256]{2,1,0:T(8,128)S(1)}) custom-call(f32[2,32,8,1024]{3,2,1,0:T(8,128)S(1)} %bitcast.7, s32[1,128]{1,0:T(1,128)S(1)} %pad_bitcast_fusion.meta, f32[2,256,256]{2,1,0:T(8,128)S(1)} %copy-done.2, s32[4,256,256]{2,1,0:T(8,128)S(1)} %bitcast.9, bf16[4,256,256]{2,1,0:T(8,128)(2,1)S(1)} %copy-done.4, ...), custom_call_target="tpu_custom_call" | custom-call | tf_op jit(solution)/shard_map/step/pallas_call | solution.py:527
  83.1 1.3 %copy.15 = f32[1,2,256,1024]{3,2,1,0:T(8,128)} copy(f32[1,2,256,1024]{3,2,1,0:T(8,128)S(1)} %bitcast.8) | data formatting | bytes 4194304
  84.4 0.6 copy.16
  (1 shorter events, 0.0 us)
Async XLA Ops:
  2.2 1.6 %copy-start = (f32[1,2,256,1024]{3,2,1,0:T(8,128)S(1)}, f32[1,2,256,1024]{3,2,1,0:T(8,128)}, u32[]{:S(2)}) copy-start(f32[1,2,256,1024]{3,2,1,0:T(8,128)} %param.8) | copy-start | bytes 6291460
  3.8 1.2 %copy-start.1 = (s32[1,1,1,4,256,256]{5,4,3,2,1,0:T(8,128)S(1)}, s32[1,1,1,4,256,256]{5,4,3,2,1,0:T(8,128)}, u32[]{:S(2)}) copy-start(s32[1,1,1,4,256,256]{5,4,3,2,1,0:T(8,128)} %param.12) | copy-start | bytes 3145732
  5.0 1.0 %copy-start.2 = (f32[2,256,256]{2,1,0:T(8,128)S(1)}, f32[2,256,256]{2,1,0:T(8,128)}, u32[]{:S(2)}) copy-start(f32[2,256,256]{2,1,0:T(8,128)} %probe_h.1) | copy-start | bytes 1572868
  6.1 1.0 %copy-start.3 = (bf16[4,256,256]{2,1,0:T(8,128)(2,1)S(1)}, bf16[4,256,256]{2,1,0:T(8,128)(2,1)}, u32[]{:S(2)}) copy-start(bf16[4,256,256]{2,1,0:T(8,128)(2,1)} %constant.9.clone.low_h) | copy-start | bytes 1572868
  7.1 1.0 %copy-start.4 = (bf16[4,256,256]{2,1,0:T(8,128)(2,1)S(1)}, bf16[4,256,256]{2,1,0:T(8,128)(2,1)}, u32[]{:S(2)}) copy-start(bf16[4,256,256]{2,1,0:T(8,128)(2,1)} %constant.8.clone.high_h) | copy-start | bytes 1572868
  8.2 0.9 %copy-start.5 = (bf16[2,256,256]{2,1,0:T(8,128)(2,1)S(1)}, bf16[2,256,256]{2,1,0:T(8,128)(2,1)}, u32[]{:S(2)}) copy-start(bf16[2,256,256]{2,1,0:T(8,128)(2,1)} %constant.10.clone.order_h) | copy-start | bytes 786436
where the time goes:
time: 85.4 us; the launch traced here: 85 us
  Pallas kernels  74 us (87%)
  local copies, waits for them, and re-layouts  9.68 us (11%)
  between operations  1.29 us (2%)
    pallas_call x1, Pallas kernels, body(): pl.pallas_call(step_kernel, name='step', out_shape=(jax.ShapeDtypeStruct(...  74 us
    unnamed x15, local copies, waits for them, and re-layouts  9.59 us

commit v1 on v0

v1 whole, which is shorter than its diff:
```python
import functools
import math

import jax
import jax.numpy as jnp
import numpy as np
from jax import lax
from jax.experimental import pallas as pl
from jax.experimental.pallas import tpu as pltpu
from jax.sharding import PartitionSpec as P

MESH = pl.DeviceIdType.MESH
F32 = jnp.float32
BF16 = jnp.bfloat16
SIZE = 256
HALF = 128
TR = 256
TC = 1024
WR = TR + SIZE
WC = TC + SIZE
N_TY = 16
N_TX = 8
N_ANGLE = 2
N_XY = N_ANGLE * N_TX


def tables():
    n = np.arange(HALF)
    base = np.exp(-2j * np.pi * np.outer(n, n) / HALF) / 16.0
    odd = base * np.exp(-2j * np.pi * n / SIZE)[None, :]

    def real_form(m):
        return np.block([[m.real, -m.imag], [m.imag, m.real]])

    mats = [real_form(base), real_form(odd)]
    mats = np.stack([mats[0], mats[1], mats[0].T, mats[1].T]).astype(np.float32)
    high = mats.astype(jnp.bfloat16)
    low = (mats - high.astype(np.float32)).astype(jnp.bfloat16)
    order = np.zeros((SIZE, SIZE), np.float32)
    for j in range(SIZE):
        order[2 * j if j < HALF else 2 * (j - HALF) + 1, j] = 1.0
    both = np.stack([order, order.T]).astype(jnp.bfloat16)
    return high, low, both


TABLE_HIGH, TABLE_LOW, TABLE_ORDER = tables()


def remote(src, dst, send, recv, **where):
    return pltpu.make_async_remote_copy(
        src_ref=src, dst_ref=dst, send_sem=send, recv_sem=recv, device_id=where, device_id_type=MESH
    )


def split(x):
    high = x.astype(BF16)
    return high, (x - high.astype(F32)).astype(BF16)


def dot(a, b):
    return jnp.dot(a, b, preferred_element_type=F32)


class Copies:
    def __init__(self, send, recv):
        self.send, self.recv, self.at = send, recv, 0

    def make(self, src, dst, **where):
        copy = remote(src, dst, self.send.at[self.at], self.recv.at[self.at], **where)
        self.at += 1
        return copy


def step_kernel(
    spots_s, live_s, tile, probe_h, counts_h, high_h, low_h, order_h, new_tile, new_probe,
    wide, probe, counts, high, low, order, around, around_s, power, padded, den, patches,
    canvas, vin, cin, hin, hout, pk_x, pk_x_in, pk_y, pk_y_in, pk, pk_z_in, pk_pair, pk_pair_in,
    den_sums, den_pair, den_mine, den_box, den_part, den_zbox, den_ybox, den_whole,
    num_sums, num_pair, num_mine, num_box, num_part, num_zbox, num_ybox, num_whole,
    send, recv, local,
):
    angle, ty, tx = lax.axis_index("angle"), lax.axis_index("ty"), lax.axis_index("tx")
    up, down = lax.rem(ty + N_TY - 1, N_TY), lax.rem(ty + 1, N_TY)
    left, right = lax.rem(tx + N_TX - 1, N_TX), lax.rem(tx + 1, N_TX)
    core, z = lax.rem(ty, 2), ty // 2
    x, y = tx // 2, 2 * angle + lax.rem(tx, 2)
    copies = Copies(send, recv)
    pair = {"ty": ty + 1 - 2 * core}

    def x_peer(step):
        other = lax.rem(x + step, 4)
        return other, {"tx": 2 * other + lax.rem(tx, 2)}

    def y_peer(step):
        other = lax.rem(y + step, 4)
        return other, {"angle": other // 2, "tx": 2 * x + lax.rem(other, 2)}

    def z_peer(step):
        other = lax.rem(z + step, 8)
        return other, {"ty": 2 * other + core}

    greeted = [{"tx": left}, {"tx": right}, {"ty": up}, {"ty": down}, pair]
    greeted += [x_peer(step)[1] for step in (1, 2, 3)] + [y_peer(step)[1] for step in (1, 2, 3)]
    greeted += [z_peer(step)[1] for step in range(1, 8)]
    barrier = pltpu.get_barrier_semaphore()
    for where in greeted:
        pl.semaphore_signal(barrier, inc=1, device_id=where, device_id_type=MESH)

    lane = lax.broadcasted_iota(jnp.int32, (1, HALF), 1)
    line = jnp.where(lane == 8, live_s[0, 0, 0], 0)
    for slot in range(4):
        for k in range(2):
            line = jnp.where(lane == 2 * slot + k, spots_s[0, 0, 0, slot, k], line)
    around[1, 1] = line

    middle_blocks, middle_groups = pl.ds(1, 8), pl.ds(16, 32)
    top_in, bottom_in = pl.ds(16, 16), pl.ds(32, 16)
    top_out, bottom_out = pl.ds(0, 16), pl.ds(48, 16)
    middle = [
        pltpu.make_async_copy(
            tile.at[:, :, :, pl.ds(block * HALF, HALF)], wide.at[1 + block, :, middle_groups], local.at[10 + block]
        )
        for block in range(8)
    ]
    loads = [
        pltpu.make_async_copy(src, dst, local.at[2 + k])
        for k, (src, dst) in enumerate(
            ((probe_h, probe), (high_h, high), (low_h, low), (order_h, order), (counts_h, counts))
        )
    ]
    for copy in middle:
        copy.start()
    for load in loads:
        load.start()

    def clear(item, carry):
        padded[item // 16, lax.rem(item // 4, 4), lax.rem(item, 4)] = jnp.zeros((96, 8, HALF), F32)
        return carry

    lax.fori_loop(0, 32, clear, 0)
    lane32 = lax.broadcasted_iota(jnp.int32, (32, 8, HALF), 2)
    lane33 = lax.broadcasted_iota(jnp.int32, (33, 8, HALF), 2)
    sub32 = lax.broadcasted_iota(jnp.int32, (32, 8, HALF), 1)
    blank = jnp.zeros((1, 8, HALF), F32)

    def lay(channel, slot, by_row, by_col, x, part_rows=0, part_cols=0):
        count = 16 if part_rows else 32
        first = 16 if part_rows == -1 else 0
        inside = lax.broadcasted_iota(jnp.int32, (count, 8, HALF), 2) >= by_col
        below = lax.broadcasted_iota(jnp.int32, (count + 1, 8, HALF), 1) >= by_row

        def turned(part):
            part = part[8 * first : 8 * (first + count)].reshape(count, 8, HALF)
            return pltpu.roll(pltpu.roll(part, by_col, 2), by_row, 1)

        zero = jnp.zeros((count, 8, HALF), F32)
        one = zero if part_cols == -1 else turned(x[:, :HALF])
        two = zero if part_cols == 1 else turned(x[:, HALF:])
        parts = (
            None if part_cols == -1 else jnp.where(inside, one, zero),
            jnp.where(inside, two, one),
            None if part_cols == 1 else jnp.where(inside, zero, two),
        )
        for step, part in enumerate(parts):
            at = padded.at[channel, slot, 1 + step]
            if part is None:
                at[pl.ds(32, 33)] = jnp.zeros((33, 8, HALF), F32)
                continue
            moved = jnp.where(
                below, jnp.concatenate([part, blank], 0), jnp.concatenate([blank, part], 0)
            )
            at[pl.ds(32 + first, count + 1)] = moved
            if part_rows == 1:
                at[pl.ds(49, 16)] = jnp.zeros((16, 8, HALF), F32)
            if part_rows == -1:
                at[pl.ds(32, 16)] = jnp.zeros((16, 8, HALF), F32)

    def fetch(channel, spots, block, first, count, put):
        where = []
        for slot in range(4):
            at_group, at_block = spots[slot]
            near = block - at_block
            where.append((jnp.where((near >= 0) & (near <= 2), near + 1, 0), 32 + first - at_group))
        for step in range(count):
            total = None
            for slot, (index, start) in enumerate(where):
                part = padded[channel, slot, index, start + step]
                total = part if total is None else total + part
            put(step, total)

    def group(dy, dx, begin):
        spots = []
        for slot in range(4):
            if begin:
                row, col, used = spots_s[0, 0, 0, slot, 0], spots_s[0, 0, 0, slot, 1], slot < live_s[0, 0, 0]
            else:
                line = around_s.at[dy + 1, dx + 1, 0]
                row, col, used = line[2 * slot], line[2 * slot + 1], slot < line[8]
            row, col = row - ty * TR, col - tx * TC
            near = (row > -SIZE) & (row < TR) & (col > -SIZE) & (col < TC)
            weight = jnp.where(used & near, 1.0, 0.0).astype(F32)
            row = jnp.clip(row, -SIZE, TR - 1) + SIZE
            col = jnp.clip(col, -SIZE, TC - 1) + SIZE
            at_group, by_row = row // 8, lax.rem(row, 8)
            at_block, by_col = col // HALF, lax.rem(col, HALF)
            lay(0, slot, by_row, by_col, power[...] * weight, dy, dx)
            spots.append((at_group - 32, at_block - 2))
        first, count = {-1: (0, 16), 0: (0, 32), 1: (16, 16)}[dy]
        begin_block, end_block = {-1: (0, 1), 0: (0, 8), 1: (7, 8)}[dx]

        def one_block(block, carry):
            def put(step, total):
                if begin:
                    den[block, first + step] = total
                else:
                    den[block, first + step] += total

            fetch(0, spots, block, first, count, put)
            return carry

        lax.fori_loop(begin_block, end_block, one_block, 0)

    loads[0].wait()
    power[...] = probe[0] * probe[0] + probe[1] * probe[1]
    for copy in middle:
        copy.wait()
    pl.semaphore_wait(barrier, len(greeted))

    meta_sides = [
        copies.make(around.at[1, 1], around.at[1, 2], tx=left),
        copies.make(around.at[1, 1], around.at[1, 0], tx=right),
    ]
    sides = [
        [
            copies.make(wide.at[1, channel, middle_groups], wide.at[9, channel, middle_groups], tx=left),
            copies.make(wide.at[8, channel, middle_groups], wide.at[0, channel, middle_groups], tx=right),
        ]
        for channel in range(2)
    ]
    ends = [
        copies.make(wide.at[middle_blocks, :, top_in], wide.at[middle_blocks, :, bottom_out], ty=up),
        copies.make(wide.at[middle_blocks, :, bottom_in], wide.at[middle_blocks, :, top_out], ty=down),
    ]
    for copy in meta_sides + sides[0] + sides[1] + ends:
        copy.start()
    for copy in meta_sides:
        copy.wait()
    meta_ends = [
        copies.make(around.at[1], around.at[2], ty=up),
        copies.make(around.at[1], around.at[0], ty=down),
    ]
    for copy in meta_ends:
        copy.start()
    group(0, 0, True)
    for copy in meta_ends:
        copy.wait()
    scalars = pltpu.make_async_copy(around, around_s, local.at[7])
    scalars.start()
    scalars.wait()

    corners = []

    def relay(channel):
        for side, block in ((0, 0), (1, 9)):
            sides[channel][1 - side].wait_recv()
            for src, dst, where in ((top_in, bottom_out, {"ty": up}), (bottom_in, top_out, {"ty": down})):
                corners.append(copies.make(wide.at[block, channel, src], wide.at[block, channel, dst], **where))
                corners[-1].start()

    for dy, dx in ((-1, 0), (1, 0)):
        group(dy, dx, False)
    relay(0)
    for dy, dx in ((0, -1), (0, 1), (-1, -1), (-1, 1)):
        group(dy, dx, False)
    relay(1)
    for dy, dx in ((1, -1), (1, 1)):
        group(dy, dx, False)
    def share(value, own, others, peers):
        own[...] = value
        sent = [copies.make(own, others.at[k], **where) for k, where in enumerate(peers)]
        for copy in sent:
            copy.start()

        def finish():
            for copy in sent:
                copy.wait()
            top = own[...]
            for k in range(len(sent)):
                top = jnp.maximum(top, others[k])
            return top

        return finish

    top_x = share(
        jnp.broadcast_to(jnp.max(den[...]), (1, HALF)), pk_x, pk_x_in, [x_peer(step)[1] for step in (1, 2, 3)]
    )
    for side in sides[0] + sides[1]:
        side.wait_send()
    for copy in ends + corners:
        copy.wait()
    top_y = share(top_x(), pk_y, pk_y_in, [y_peer(step)[1] for step in (1, 2, 3)])

    den_sums[...] = jnp.zeros_like(den_sums)
    num_sums[...] = jnp.zeros_like(num_sums)

    def place_of(slot):
        row = jnp.clip(spots_s[0, 0, 0, slot, 0] - (ty * TR - HALF), 0, TR - 1)
        col = jnp.clip(spots_s[0, 0, 0, slot, 1] - (tx * TC - HALF), 0, TC - 1)
        return row // 8, lax.rem(row, 8), col // HALF, lax.rem(col, HALF)

    def weight_of(slot):
        return jnp.where(slot < live_s[0, 0, 0], 1.0, 0.0).astype(F32)

    def add_rows(sums, channel, value):
        value = value.reshape(8, 2, 2, 8, SIZE)
        for parity in range(2):
            for quarter in range(4):
                side = HALF * (quarter % 2)
                sums[parity, quarter, :, channel] += value[:, parity, quarter // 2, :, side : side + HALF]

    def cut(slot, carry):
        at_group, by_row, at_block, by_col = place_of(slot)
        back_row, back_col = lax.rem(8 - by_row, 8), lax.rem(HALF - by_col, HALF)
        square = None
        for channel in range(2):
            parts = []
            for step in range(3):
                x = jnp.stack([wide[at_block + step, channel, at_group + k] for k in range(33)])
                parts.append(pltpu.roll(x, back_col, 2))
            done = []
            for step in range(2):
                x = jnp.where(lane33 < HALF - by_col, parts[step], parts[step + 1])
                x = pltpu.roll(x, back_row, 1)
                x = jnp.where(sub32 < 8 - by_row, x[:32], x[1:])
                done.append(x.reshape(SIZE, HALF))
            x = jnp.concatenate(done, 1)
            patches[slot, channel] = x
            square = x * x if square is None else square + x * x
        add_rows(den_sums, 0, square * weight_of(slot))
        return carry

    lax.fori_loop(0, 4, cut, 0)

    class Chain:
        def __init__(self, sums, pair_in, mine, box, part, zbox, ybox, whole):
            self.__dict__.update(sums=sums, pair_in=pair_in, mine=mine, box=box, part=part, zbox=zbox, ybox=ybox, whole=whole)
            self.over_pair = copies.make(sums.at[1 - core], pair_in, **pair)
            self.over_x = [
                copies.make(mine.at[x_peer(step)[0]], box.at[step], **x_peer(step)[1]) for step in (1, 2, 3)
            ]
            self.over_z = [
                copies.make(part.at[z_peer(step)[0]], zbox.at[step], **z_peer(step)[1]) for step in range(1, 8)
            ]
            self.over_y = [copies.make(ybox.at[y], ybox.at[y], **y_peer(step)[1]) for step in (1, 2, 3)]
            self.out = [copies.make(whole.at[x], whole.at[x], **x_peer(step)[1]) for step in (1, 2, 3)]

        def start_pair(self):
            self.over_pair.start()

        def start_x(self):
            self.over_pair.wait()
            self.mine[...] = self.sums[core] + self.pair_in[...]
            for copy in self.over_x:
                copy.start()

        def start_z(self):
            for copy in self.over_x:
                copy.wait()
            self.part[...] = self.mine[x] + self.box[1] + self.box[2] + self.box[3]
            for copy in self.over_z:
                copy.start()

        def start_y(self):
            for copy in self.over_z:
                copy.wait()
            total = self.part[z]
            for step in range(1, 8):
                total = total + self.zbox[step]
            self.ybox[y] = total
            for copy in self.over_y:
                copy.start()

        def start_out(self):
            for copy in self.over_y:
                copy.wait()
            self.whole[x] = (self.ybox[0] + self.ybox[1]) + (self.ybox[2] + self.ybox[3])
            for copy in self.out:
                copy.start()

        def finish(self):
            for copy in self.out:
                copy.wait()

    den_chain = Chain(den_sums, den_pair, den_mine, den_box, den_part, den_zbox, den_ybox, den_whole)
    num_chain = Chain(num_sums, num_pair, num_mine, num_box, num_part, num_zbox, num_ybox, num_whole)
    den_chain.start_pair()
    for load in loads[1:]:
        load.wait()

    def from_left(which, x):
        a, b = split(x)
        return dot(high[which], a) + (dot(high[which], b) + dot(low[which], a))

    def from_right(x, which):
        a, b = split(x)
        return dot(a, high[which]) + (dot(b, high[which]) + dot(a, low[which]))

    def one_slot(slot, carry):
        at_group, by_row, at_block, by_col = place_of(slot)
        weight = weight_of(slot)
        xr, xi = patches[slot, 0], patches[slot, 1]
        qr, qi = probe[0], probe[1]
        pr, pi = qr * xr - qi * xi, qr * xi + qi * xr
        even = from_right(
            jnp.concatenate([pr[:, :HALF] + pr[:, HALF:], pi[:, :HALF] + pi[:, HALF:]], 1), 2
        )
        odd = from_right(
            jnp.concatenate([pr[:, :HALF] - pr[:, HALF:], pi[:, :HALF] - pi[:, HALF:]], 1), 3
        )
        mr = jnp.concatenate([even[:, :HALF], odd[:, :HALF]], 1)
        mi = jnp.concatenate([even[:, HALF:], odd[:, HALF:]], 1)
        fe = from_left(0, jnp.concatenate([mr[:HALF] + mr[HALF:], mi[:HALF] + mi[HALF:]], 0))
        fo = from_left(1, jnp.concatenate([mr[:HALF] - mr[HALF:], mi[:HALF] - mi[HALF:]], 0))
        count = counts[slot]
        tens = lax.shift_right_logical(count, 4)
        ones = count - 16 * tens
        tens = dot(dot(order[1], tens.astype(F32).astype(BF16)).astype(BF16), order[0])
        ones = dot(dot(order[1], ones.astype(F32).astype(BF16)).astype(BF16), order[0])
        count = 16.0 * tens + ones

        def scaled(f, c):
            re, im = f[:HALF], f[HALF:]
            size = jnp.maximum(re * re + im * im, 0.0625)
            factor = (0.05 * c) * lax.rsqrt(c * size)
            return jnp.concatenate([re * factor, im * factor], 0)

        ge = from_left(2, scaled(fe, count[:HALF]))
        go = from_left(3, scaled(fo, count[HALF:]))
        top, bottom = ge + go, ge - go
        hr_ = jnp.concatenate([top[:HALF], bottom[:HALF]], 0)
        hi_ = jnp.concatenate([top[HALF:], bottom[HALF:]], 0)
        be = from_right(jnp.concatenate([hr_[:, :HALF], hi_[:, :HALF]], 1), 0)
        bo = from_right(jnp.concatenate([hr_[:, HALF:], hi_[:, HALF:]], 1), 1)
        first, second = be + bo, be - bo
        dr = (jnp.concatenate([first[:, :HALF], second[:, :HALF]], 1) - pr) * weight
        di = (jnp.concatenate([first[:, HALF:], second[:, HALF:]], 1) - pi) * weight
        lay(0, slot, by_row, by_col, qr * dr + qi * di)
        lay(1, slot, by_row, by_col, qr * di - qi * dr)
        add_rows(num_sums, 0, xr * dr + xi * di)
        add_rows(num_sums, 1, xr * di - xi * dr)
        return carry

    lax.fori_loop(0, 1, one_slot, 0)
    den_chain.start_x()
    lax.fori_loop(1, 3, one_slot, 0)
    den_chain.start_z()
    lax.fori_loop(3, 4, one_slot, 0)
    num_chain.start_pair()

    places = [(place_of(slot)[0], place_of(slot)[2]) for slot in range(4)]

    def one_canvas(first, count):
        def add(block, carry):
            for channel in range(2):
                def put(step, total):
                    canvas[block, channel, first + step] = total

                fetch(channel, places, block, first, count, put)
            return carry

        return add

    lax.fori_loop(0, 2, lambda k, carry: one_canvas(0, 64)(9 * k, carry), 0)
    back_corners = []
    for side, block in ((0, 0), (1, 9)):
        for way, (src, where) in enumerate(((top_out, {"ty": up}), (bottom_out, {"ty": down}))):
            back_corners.append(copies.make(canvas.at[block, :, src], cin.at[2 * side + way], **where))
            back_corners[-1].start()
    num_chain.start_x()
    den_chain.start_y()
    lax.fori_loop(1, 9, one_canvas(0, 16), 0)
    lax.fori_loop(1, 9, one_canvas(48, 16), 0)
    back_ends = []
    for channel in range(2):
        for part in range(2):
            blocks, there = pl.ds(1 + 4 * part, 4), pl.ds(4 * part, 4)
            back_ends.append(
                [
                    copies.make(canvas.at[blocks, channel, top_out], vin.at[0, channel, there], ty=up),
                    copies.make(canvas.at[blocks, channel, bottom_out], vin.at[1, channel, there], ty=down),
                ]
            )

    def start_ends(k):
        for copy in back_ends[k]:
            copy.start()

    start_ends(0)
    den_chain.start_out()
    for copy in back_corners:
        copy.wait()
    for side, block in ((0, 0), (1, 9)):
        hout[side, :, pl.ds(0, 16)] = canvas[block, :, top_in] + cin[2 * side + 1]
        hout[side, :, pl.ds(16, 16)] = canvas[block, :, bottom_in] + cin[2 * side]
    across = [
        copies.make(hout.at[0], hin.at[0], tx=left),
        copies.make(hout.at[1], hin.at[1], tx=right),
    ]
    for copy in across:
        copy.start()
    start_ends(1)
    num_chain.start_z()
    den_chain.finish()
    pk[0] = top_y()
    pk[1] = jnp.broadcast_to(jnp.max(den_whole[...]), (1, HALF))
    top_z = share(pk[...], pk, pk_z_in, [z_peer(step)[1] for step in range(1, 8)])
    start_ends(2)
    lax.fori_loop(1, 9, one_canvas(16, 32), 0)
    num_chain.start_y()
    start_ends(3)
    top_pair = share(top_z(), pk_pair, pk_pair_in, [pair])
    num_chain.start_out()
    top = top_pair()
    peak_obj, peak_probe = top[0, 0, 0], top[1, 0, 0]
    den[...] = 1.0 / (den[...] + 0.1 * peak_obj)
    for copy in across:
        copy.wait()
    for block, side in ((8, 0), (1, 1)):
        canvas[block, :, middle_groups] += hin[side]
    for channel in range(2):
        for copy in back_ends[2 * channel] + back_ends[2 * channel + 1]:
            copy.wait()
        for first, side in ((0, 1), (16, 0)):
            here, there = pl.ds(16 + first, 16), pl.ds(first, 16)
            for block in range(8):
                value = canvas[1 + block, channel, here] + vin[side, channel, block]
                new_tile[channel, there, :, pl.ds(block * HALF, HALF)] = (
                    wide[1 + block, channel, here] + value * den[block, there]
                )
    num_chain.finish()
    for quarter in range(4):
        rows = pl.ds(pl.multiple_of(16 * ty + 8 * (quarter // 2), 8), 8)
        cols = pl.ds(HALF * (quarter % 2), HALF)
        scale = 1.0 / (den_whole[quarter, 0] + 0.1 * peak_probe)
        for channel in range(2):
            new_probe[channel, pl.ds(8 * (quarter // 2), 8), cols] = (
                probe[channel, rows, cols] + num_whole[quarter, channel] * scale
            )


def vmem():
    return pl.BlockSpec(memory_space=pltpu.VMEM)


def chain_scratch(channels):
    piece = (channels, 8, HALF)
    shapes = (
        (2, 4, 8) + piece, (4, 8) + piece, (4, 8) + piece, (4, 8) + piece,
        (8,) + piece, (8,) + piece, (4,) + piece, (4,) + piece,
    )
    return [pltpu.VMEM(shape, F32) for shape in shapes]


def body(object_slices, probe_field, positions, live_slots, photon_counts):
    new_tile, new_probe = pl.pallas_call(
        step_kernel,
        name="step",
        out_shape=(
            jax.ShapeDtypeStruct((2, 32, 8, TC), F32),
            jax.ShapeDtypeStruct((2, 16, SIZE), F32),
        ),
        in_specs=[pl.BlockSpec(memory_space=pltpu.SMEM)] * 2 + [pl.BlockSpec(memory_space=pltpu.HBM)] * 6,
        out_specs=(vmem(), vmem()),
        scratch_shapes=[
            pltpu.VMEM((10, 2, 64, 8, HALF), F32),
            pltpu.VMEM((2, SIZE, SIZE), F32),
            pltpu.VMEM((4, SIZE, SIZE), jnp.int32),
            pltpu.VMEM((4, SIZE, SIZE), BF16),
            pltpu.VMEM((4, SIZE, SIZE), BF16),
            pltpu.VMEM((2, SIZE, SIZE), BF16),
            pltpu.VMEM((3, 3, 1, HALF), jnp.int32),
            pltpu.SMEM((3, 3, 1, HALF), jnp.int32),
            pltpu.VMEM((SIZE, SIZE), F32),
            pltpu.VMEM((2, 4, 4, 96, 8, HALF), F32),
            pltpu.VMEM((8, 32, 8, HALF), F32),
            pltpu.VMEM((4, 2, SIZE, SIZE), F32),
            pltpu.VMEM((10, 2, 64, 8, HALF), F32),
            pltpu.VMEM((2, 2, 8, 16, 8, HALF), F32),
            pltpu.VMEM((4, 2, 16, 8, HALF), F32),
            pltpu.VMEM((2, 2, 32, 8, HALF), F32),
            pltpu.VMEM((2, 2, 32, 8, HALF), F32),
            pltpu.VMEM((1, HALF), F32),
            pltpu.VMEM((3, 1, HALF), F32),
            pltpu.VMEM((1, HALF), F32),
            pltpu.VMEM((3, 1, HALF), F32),
            pltpu.VMEM((2, 1, HALF), F32),
            pltpu.VMEM((7, 2, 1, HALF), F32),
            pltpu.VMEM((2, 1, HALF), F32),
            pltpu.VMEM((1, 2, 1, HALF), F32),
            *chain_scratch(1),
            *chain_scratch(2),
            pltpu.SemaphoreType.DMA((152,)),
            pltpu.SemaphoreType.DMA((152,)),
            pltpu.SemaphoreType.DMA((18,)),
        ],
        compiler_params=pltpu.CompilerParams(
            collective_id=0, has_side_effects=True, vmem_limit_bytes=56 << 20
        ),
    )(
        positions, live_slots, object_slices.reshape(2, 32, 8, TC), probe_field, photon_counts[0, 0, 0],
        jnp.asarray(TABLE_HIGH), jnp.asarray(TABLE_LOW), jnp.asarray(TABLE_ORDER),
    )
    return (new_tile.reshape(1, 2, TR, TC), new_probe)


def solution(mesh):
    placed = (
        P("angle", None, "ty", "tx"),
        P(),
        P("angle", "ty", "tx", None, None),
        P("angle", "ty", "tx"),
        P("angle", "ty", "tx", None, None, None),
    )
    return jax.shard_map(
        body,
        mesh=mesh,
        in_specs=placed,
        out_specs=(P("angle", None, "ty", "tx"), P(None, "ty", None)),
        check_vma=False,
    )
```

time: 85.4 us -> 75.1 us (0.88)
  Pallas kernels: 74 us -> 68.5 us
  local copies, waits for them, and re-layouts: 9.68 us -> 5.12 us
    pallas_call x1, Pallas kernels: 74 us -> 68.5 us  [body(): pl.pallas_call(step_kernel, name='step', out_shape=(jax.ShapeDtypeStruct(...]
    unnamed x15 -> x5, local copies, waits for them, and re-layouts: 9.59 us -> 5.12 us
where the time goes in v1:
time: 75.1 us; the launch traced here: 74.9 us
  Pallas kernels  68.5 us (91%)
  local copies, waits for them, and re-layouts  5.12 us (7%)
  between operations  1.29 us (2%)
    pallas_call x1, Pallas kernels, body(): pl.pallas_call(step_kernel, name='step', out_shape=(jax.ShapeDtypeStruct(...  68.5 us
    unnamed x5, local copies, waits for them, and re-layouts  5.12 us

profile of v1, /device:TPU:1, one launch (start us, length us, event | category | flops | bytes accessed | tf_op | source)
XLA Modules:
  0.0 74.9 jit_solution(3034532079336714760)
XLA Ops:
  1.3 1.3 %copy.10.spots_s = s32[1,1,1,4,2]{4,3,2,1,0:T(4,128)} copy(s32[1,1,1,4,2]{3,4,2,1,0:T(2,128)} %param.10) | data formatting | bytes 64 | tf_op args[2]
  2.6 68.5 %step.1 = (f32[2,32,8,1024]{3,2,1,0:T(8,128)}, f32[2,16,256]{2,1,0:T(8,128)}) custom-call(s32[1,1,1,4,2]{4,3,2,1,0:T(4,128)} %copy.10.spots_s, s32[1,1,1]{2,1,0:T(1,128)S(6)} %copy.13.live_s, f32[2,32,8,1024]{3,2,1,0:T(8,128)} %bitcast.3, f32[2,256,256]{2,1,0:T(8,128)} %probe_h.1, s32[4,256,256]{2,1,0:T(8,128)} %bitcast.5, ...), custom_call_target="tpu_custom_call" | custom-call | tf_op jit(solution)/shard_map/step/pallas_call | solution.py:565
  71.1 0.0 copy-start
  71.1 3.2 %copy.14 = f32[1,2,256,1024]{3,2,1,0:T(8,128)} copy(f32[1,2,256,1024]{3,2,1,0:T(8,128)} %bitcast.4) | data formatting | bytes 4194304
  74.3 0.0 copy-done
  74.3 0.6 copy.15
Async XLA Ops:
  71.1 3.2 %copy-start = (f32[2,16,256]{2,1,0:T(8,128)S(1)}, f32[2,16,256]{2,1,0:T(8,128)}, u32[]{:S(2)}) copy-start(f32[2,16,256]{2,1,0:T(8,128)} %get-tuple-element.9) | copy-start | bytes 98308

commit v2 on v1

--- a/solution.py
+++ b/solution.py
@@ -43,7 +43,7 @@
     return high, low, both
 
 
-TABLE_HIGH, TABLE_LOW, TABLE_ORDER = tables()
+TABLES = np.concatenate(tables())
 
 
 def remote(src, dst, send, recv, **where):
@@ -72,8 +72,8 @@
 
 
 def step_kernel(
-    spots_s, live_s, tile, probe_h, counts_h, high_h, low_h, order_h, new_tile, new_probe,
-    wide, probe, counts, high, low, order, around, around_s, power, padded, den, patches,
+    spots_s, live_s, tile, probe_h, counts_h, tables_h, new_tile, new_probe,
+    wide, probe, counts, tables_v, around, around_s, power, padded, den, patches,
     canvas, vin, cin, hin, hout, pk_x, pk_x_in, pk_y, pk_y_in, pk, pk_z_in, pk_pair, pk_pair_in,
     den_sums, den_pair, den_mine, den_box, den_part, den_zbox, den_ybox, den_whole,
     num_sums, num_pair, num_mine, num_box, num_part, num_zbox, num_ybox, num_whole,
@@ -85,6 +85,7 @@
     core, z = lax.rem(ty, 2), ty // 2
     x, y = tx // 2, 2 * angle + lax.rem(tx, 2)
     copies = Copies(send, recv)
+    high, low, order = (tables_v.at[pl.ds(at, n)] for at, n in ((0, 4), (4, 4), (8, 2)))
     pair = {"ty": ty + 1 - 2 * core}
 
     def x_peer(step):
@@ -125,13 +126,12 @@
     loads = [
         pltpu.make_async_copy(src, dst, local.at[2 + k])
         for k, (src, dst) in enumerate(
-            ((probe_h, probe), (high_h, high), (low_h, low), (order_h, order), (counts_h, counts))
+            ((probe_h, probe), (tables_h, tables_v), (counts_h, counts))
         )
     ]
     for copy in middle:
         copy.start()
-    for load in loads:
-        load.start()
+    loads[0].start()
 
     def clear(item, carry):
         padded[item // 16, lax.rem(item // 4, 4), lax.rem(item, 4)] = jnp.zeros((96, 8, HALF), F32)
@@ -243,6 +243,8 @@
     ]
     for copy in meta_sides + sides[0] + sides[1] + ends:
         copy.start()
+    for load in loads[1:]:
+        load.start()
     for copy in meta_sides:
         copy.wait()
     meta_ends = [
@@ -270,10 +272,10 @@
     for dy, dx in ((-1, 0), (1, 0)):
         group(dy, dx, False)
     relay(0)
-    for dy, dx in ((0, -1), (0, 1), (-1, -1), (-1, 1)):
+    for dy, dx in ((0, -1), (0, 1)):
         group(dy, dx, False)
     relay(1)
-    for dy, dx in ((1, -1), (1, 1)):
+    for dy, dx in ((-1, -1), (-1, 1), (1, -1), (1, 1)):
         group(dy, dx, False)
     def share(value, own, others, peers):
         own[...] = value
@@ -450,11 +452,12 @@
         add_rows(num_sums, 1, xr * di - xi * dr)
         return carry
 
-    lax.fori_loop(0, 1, one_slot, 0)
+    one_slot(0, 0)
     den_chain.start_x()
-    lax.fori_loop(1, 3, one_slot, 0)
+    one_slot(1, 0)
+    one_slot(2, 0)
     den_chain.start_z()
-    lax.fori_loop(3, 4, one_slot, 0)
+    one_slot(3, 0)
     num_chain.start_pair()
 
     places = [(place_of(slot)[0], place_of(slot)[2]) for slot in range(4)]
@@ -523,20 +526,25 @@
     top = top_pair()
     peak_obj, peak_probe = top[0, 0, 0], top[1, 0, 0]
     den[...] = 1.0 / (den[...] + 0.1 * peak_obj)
-    for copy in across:
+    for copy in [copy for both in back_ends for copy in both]:
         copy.wait()
-    for block, side in ((8, 0), (1, 1)):
-        canvas[block, :, middle_groups] += hin[side]
-    for channel in range(2):
-        for copy in back_ends[2 * channel] + back_ends[2 * channel + 1]:
-            copy.wait()
-        for first, side in ((0, 1), (16, 0)):
-            here, there = pl.ds(16 + first, 16), pl.ds(first, 16)
-            for block in range(8):
+
+    def update(block):
+        for channel in range(2):
+            for first, side in ((0, 1), (16, 0)):
+                here, there = pl.ds(16 + first, 16), pl.ds(first, 16)
                 value = canvas[1 + block, channel, here] + vin[side, channel, block]
                 new_tile[channel, there, :, pl.ds(block * HALF, HALF)] = (
                     wide[1 + block, channel, here] + value * den[block, there]
                 )
+
+    for block in range(1, 7):
+        update(block)
+    for copy in across:
+        copy.wait()
+    for block, side in ((7, 0), (0, 1)):
+        canvas[1 + block, :, middle_groups] += hin[side]
+        update(block)
     num_chain.finish()
     for quarter in range(4):
         rows = pl.ds(pl.multiple_of(16 * ty + 8 * (quarter // 2), 8), 8)
@@ -569,15 +577,13 @@
             jax.ShapeDtypeStruct((2, 32, 8, TC), F32),
             jax.ShapeDtypeStruct((2, 16, SIZE), F32),
         ),
-        in_specs=[pl.BlockSpec(memory_space=pltpu.SMEM)] * 2 + [pl.BlockSpec(memory_space=pltpu.HBM)] * 6,
+        in_specs=[pl.BlockSpec(memory_space=pltpu.SMEM)] * 2 + [pl.BlockSpec(memory_space=pltpu.HBM)] * 4,
         out_specs=(vmem(), vmem()),
         scratch_shapes=[
             pltpu.VMEM((10, 2, 64, 8, HALF), F32),
             pltpu.VMEM((2, SIZE, SIZE), F32),
             pltpu.VMEM((4, SIZE, SIZE), jnp.int32),
-            pltpu.VMEM((4, SIZE, SIZE), BF16),
-            pltpu.VMEM((4, SIZE, SIZE), BF16),
-            pltpu.VMEM((2, SIZE, SIZE), BF16),
+            pltpu.VMEM((10, SIZE, SIZE), BF16),
             pltpu.VMEM((3, 3, 1, HALF), jnp.int32),
             pltpu.SMEM((3, 3, 1, HALF), jnp.int32),
             pltpu.VMEM((SIZE, SIZE), F32),
@@ -604,11 +610,11 @@
             pltpu.SemaphoreType.DMA((18,)),
         ],
         compiler_params=pltpu.CompilerParams(
-            collective_id=0, has_side_effects=True, vmem_limit_bytes=56 << 20
+            collective_id=0, has_side_effects=True, vmem_limit_bytes=48 << 20
         ),
     )(
         positions, live_slots, object_slices.reshape(2, 32, 8, TC), probe_field, photon_counts[0, 0, 0],
-        jnp.asarray(TABLE_HIGH), jnp.asarray(TABLE_LOW), jnp.asarray(TABLE_ORDER),
+        jnp.asarray(TABLES),
     )
     return (new_tile.reshape(1, 2, TR, TC), new_probe)
 

time: 75.1 us -> 74.7 us (level)
  Pallas kernels: 68.5 us -> 66.8 us
  local copies, waits for them, and re-layouts: 5.12 us -> 6.28 us
    pallas_call x1, Pallas kernels: 68.5 us -> 66.8 us  [body(): pl.pallas_call(step_kernel, name='step', out_shape=(jax.ShapeDtypeStruct(...]
    unnamed x5 -> x9, local copies, waits for them, and re-layouts: 5.12 us -> 6.28 us
where the time goes in v2:
time: 74.7 us; the launch traced here: 74.4 us
  Pallas kernels  66.8 us (89%)
  local copies, waits for them, and re-layouts  6.28 us (8%)
  between operations  1.29 us (2%)
    pallas_call x1, Pallas kernels, body(): pl.pallas_call(step_kernel, name='step', out_shape=(jax.ShapeDtypeStruct(...  66.8 us
    unnamed x9, local copies, waits for them, and re-layouts  6.28 us

profile of v2, /device:TPU:1, one launch (start us, length us, event | category | flops | bytes accessed | tf_op | source)
XLA Modules:
  0.0 74.4 jit_solution(8724447631043287446)
XLA Ops:
  1.3 0.8 %copy.8.spots_s = s32[1,1,1,4,2]{4,3,2,1,0:T(4,128)S(1)} copy(s32[1,1,1,4,2]{3,4,2,1,0:T(2,128)} %param.8) | data formatting | bytes 64 | tf_op args[2]
  2.0 0.0 copy-start
  2.0 1.3 %copy-done = bf16[10,256,256]{2,1,0:T(8,128)(2,1)S(1)} copy-done((bf16[10,256,256]{2,1,0:T(8,128)(2,1)S(1)}, bf16[10,256,256]{2,1,0:T(8,128)(2,1)}, u32[]{:S(2)}) %copy-start) | copy-done | bytes 1310744
  3.4 0.0 copy-start.1
  3.4 1.2 %copy-done.1 = s32[1,1,1,4,256,256]{5,4,3,2,1,0:T(8,128)S(1)} copy-done((s32[1,1,1,4,256,256]{5,4,3,2,1,0:T(8,128)S(1)}, s32[1,1,1,4,256,256]{5,4,3,2,1,0:T(8,128)}, u32[]{:S(2)}) %copy-start.1) | copy-done | bytes 1048600
  4.6 0.0 copy-start.2
  4.6 1.0 %copy-done.2 = f32[2,256,256]{2,1,0:T(8,128)S(1)} copy-done((f32[2,256,256]{2,1,0:T(8,128)S(1)}, f32[2,256,256]{2,1,0:T(8,128)}, u32[]{:S(2)}) %copy-start.2) | copy-done | bytes 524312
  5.6 66.8 %step.1 = (f32[2,32,8,1024]{3,2,1,0:T(8,128)S(1)}, f32[2,16,256]{2,1,0:T(8,128)S(1)}) custom-call(s32[1,1,1,4,2]{4,3,2,1,0:T(4,128)S(1)} %copy.8.spots_s, s32[1,1,1]{2,1,0:T(1,128)S(6)} %copy.11.live_s, f32[2,32,8,1024]{3,2,1,0:T(8,128)} %bitcast.5, f32[2,256,256]{2,1,0:T(8,128)S(1)} %copy-done.2, s32[4,256,256]{2,1,0:T(8,128)S(1)} %bitcast.4, ...), custom_call_target="tpu_custom_call" | custom-call | tf_op jit(solution)/shard_map/step/pallas_call | solution.py:573
  72.5 1.3 %copy.12 = f32[1,2,256,1024]{3,2,1,0:T(8,128)} copy(f32[1,2,256,1024]{3,2,1,0:T(8,128)S(1)} %bitcast.3) | data formatting | bytes 4194304
  73.8 0.6 copy.13
Async XLA Ops:
  2.0 1.3 %copy-start = (bf16[10,256,256]{2,1,0:T(8,128)(2,1)S(1)}, bf16[10,256,256]{2,1,0:T(8,128)(2,1)}, u32[]{:S(2)}) copy-start(bf16[10,256,256]{2,1,0:T(8,128)(2,1)} %constant.2.clone.tables_h) | copy-start | bytes 3932164
  3.4 1.2 %copy-start.1 = (s32[1,1,1,4,256,256]{5,4,3,2,1,0:T(8,128)S(1)}, s32[1,1,1,4,256,256]{5,4,3,2,1,0:T(8,128)}, u32[]{:S(2)}) copy-start(s32[1,1,1,4,256,256]{5,4,3,2,1,0:T(8,128)} %param.10) | copy-start | bytes 3145732
  4.6 1.0 %copy-start.2 = (f32[2,256,256]{2,1,0:T(8,128)S(1)}, f32[2,256,256]{2,1,0:T(8,128)}, u32[]{:S(2)}) copy-start(f32[2,256,256]{2,1,0:T(8,128)} %probe_h.1) | copy-start | bytes 1572868
